TPU v7x, 32 devices: a whole 2x2x4 slice. The times are simulated.
32 devices in a mesh: dom: 8 (over z, y), sub: 4 (over x, core).
Axes of the slice: x: 2, y: 2, z: 4, core: 2. Of those that a mesh axis runs over, the one named last changes fastest.
Arguments:
- node_state: bfloat16 [64, 32768], P(None, ('dom', 'sub')), may hold values from -6 to 6
- edge_state: bfloat16 [64, 98304], P(None, ('dom', 'sub')), may hold values from -6 to 6
- senders: int32 [98304], P(('dom', 'sub')), may hold values from 0 to 2559, as said below
- receivers: int32 [98304], P(('dom', 'sub')), may hold values from 0 to 1023
- send_index: int32 [32, 12, 128], P(('dom', 'sub')), may hold values from -1 to 1023, as said below
- node_cotangent: bfloat16 [64, 32768], P(None, ('dom', 'sub')), may hold values from -6 to 6
- edge_cotangent: bfloat16 [64, 98304], P(None, ('dom', 'sub')), may hold values from -6 to 6
- edge_first: bfloat16 [192, 64], replicated, may hold values from -0.4375 to 0.4375
- edge_bias: float32 [64], replicated, may hold values from -3 to 3
- edge_second: bfloat16 [64, 64], replicated, may hold values from -0.75 to 0.75
- edge_gain: float32 [64], replicated, may hold values from 0.1 to 1.9
- edge_shift: float32 [64], replicated, may hold values from -3 to 3
- node_first: bfloat16 [128, 64], replicated, may hold values from -0.5 to 0.5
- node_bias: float32 [64], replicated, may hold values from -3 to 3
- node_second: bfloat16 [64, 64], replicated, may hold values from -0.75 to 0.75
- node_gain: float32 [64], replicated, may hold values from 0.1 to 1.9
Outputs:
- delta_state: bfloat16 [64, 32768], P(None, ('dom', 'sub'))
- delta_edges: bfloat16 [64, 98304], P(None, ('dom', 'sub'))
- delta_edgefirst: float32 [192, 64], replicated
- delta_edgebias: float32 [64], replicated
- delta_edgesecond: float32 [64, 64], replicated
- delta_edgegain: float32 [64], replicated
- delta_edgeshift: float32 [64], replicated
- delta_nodefirst: float32 [128, 64], replicated
- delta_nodebias: float32 [64], replicated
- delta_nodesecond: float32 [64, 64], replicated
- delta_nodegain: float32 [64], replicated
- delta_nodeshift: float32 [64], replicated
Inputs may be any that keep to these rules, and one draw needn't show every extreme that they name: `send_index`: block k = o * 4 + t of partition p = d * 4 + s lists own cells that p sends to the partition at dom index d + o - 1 and sub index t: live entries first, then -1. Blocks towards a dom index outside the mesh, and block 4 + s, hold only -1; every other block holds 32 to 128 live entries. Some partition receives a full block from every partition that sends to it. `senders`: an entry below 1024 is an own cell. An entry 1024 + k * 128 + j with k = o * 4 + u names ghost slot j of block k: the j-th entry of block o * 4 + s of the partition at dom index d + 1 - o and sub index u, and that entry is live.
All inputs are finite; a program needn't handle non-finite values.
Results may differ from a plain program's by a relative error of at most 0.0095.
Values may be sent and summed in bfloat16 or wider, within the bound.
A program may use at most 64 MiB of HBM per device.

v0:
```python
import math
import jax
import jax.numpy as jnp
from jax import lax
from jax.sharding import PartitionSpec as P

EPSILON = 1e-05


def from_behind(value, axis, steps):
    count = lax.axis_size(axis)
    first, last = (max(0, -steps), min(count, count - steps))
    return lax.ppermute(value, axis, [(source, source + steps) for source in range(first, last)])


def contract_first(first_operand, second_operand):
    return lax.dot_general(
        first_operand, second_operand, (((0,), (0,)), ((), ())), preferred_element_type=jnp.float32
    )


def contract_last(first_operand, second_operand):
    return lax.dot_general(
        first_operand, second_operand, (((1,), (1,)), ((), ())), preferred_element_type=jnp.float32
    )


def sigmoid_linear(values):
    return values * jax.nn.sigmoid(values)


def sigmoid_slope(values):
    logistic = jax.nn.sigmoid(values)
    return logistic * (1.0 + values * (1.0 - logistic))


def standardize(values):
    centered = values - jnp.mean(values, axis=0, keepdims=True)
    spread = lax.rsqrt(jnp.mean(centered * centered, axis=0, keepdims=True) + EPSILON)
    return (centered * spread, spread)


def normalize_back(upstream, scaled, spread, gain_vector):
    gain_delta = jnp.sum(upstream * scaled, axis=1)
    shift_delta = jnp.sum(upstream, axis=1)
    weighted = upstream * gain_vector[:, None]
    result = spread * (
        weighted
        - jnp.mean(weighted, axis=0, keepdims=True)
        - scaled * jnp.mean(weighted * scaled, axis=0, keepdims=True)
    )
    return (result, gain_delta, shift_delta)


def block_sizes(count, width):
    step = math.gcd(count, 512)
    piece = math.gcd(width, 2048)
    return (step, piece)


def pick_precision(values):
    if values.dtype == jnp.float32:
        return lax.Precision.HIGHEST
    return None


def column_gather(table, index):
    rows, width = table.shape
    count = index.shape[0]
    step, piece = block_sizes(count, width)
    blocks = index.reshape(count // step, step)
    precision = pick_precision(table)

    def one_block(number, result):
        chosen = lax.dynamic_index_in_dim(blocks, number, 0, keepdims=False)
        total = jnp.zeros((rows, step), jnp.float32)
        for begin in range(0, width, piece):
            columns = lax.iota(jnp.int32, piece) + begin
            selector = (columns[:, None] == chosen[None, :]).astype(table.dtype)
            total = total + jnp.dot(
                table[:, begin : begin + piece],
                selector,
                precision=precision,
                preferred_element_type=jnp.float32,
            )
        return lax.dynamic_update_slice_in_dim(result, total.astype(table.dtype), number * step, 1)

    return lax.fori_loop(0, count // step, one_block, jnp.zeros((rows, count), table.dtype))


def column_scatter(values, index, width):
    rows, count = values.shape
    step, piece = block_sizes(count, width)
    blocks = index.reshape(count // step, step)
    precision = pick_precision(values)

    def one_block(number, result):
        chosen = lax.dynamic_index_in_dim(blocks, number, 0, keepdims=False)
        portion = lax.dynamic_slice_in_dim(values, number * step, step, 1)
        pieces = []
        for begin in range(0, width, piece):
            columns = lax.iota(jnp.int32, piece) + begin
            selector = (chosen[:, None] == columns[None, :]).astype(values.dtype)
            pieces.append(
                jnp.dot(portion, selector, precision=precision, preferred_element_type=jnp.float32)
            )
        return result + jnp.concatenate(pieces, axis=1)

    return lax.fori_loop(0, count // step, one_block, jnp.zeros((rows, width), jnp.float32))


def local_backward(
    extended,
    node_state,
    edge_state,
    senders,
    receivers,
    node_cotangent,
    edge_cotangent,
    edge_first,
    edge_bias,
    edge_second,
    edge_gain,
    edge_shift,
    node_first,
    node_bias,
    node_second,
    node_gain,
):
    features, cell_count = node_state.shape
    sender_rows = column_gather(extended, senders)
    receiver_rows = column_gather(node_state, receivers)
    stacked = jnp.concatenate([sender_rows, receiver_rows, edge_state], axis=0)
    edge_linear = contract_first(edge_first, stacked) + edge_bias[:, None]
    edge_active = sigmoid_linear(edge_linear).astype(jnp.bfloat16)
    edge_output = contract_first(edge_second, edge_active)
    edge_scaled, edge_spread = standardize(edge_output)
    message = (edge_scaled * edge_gain[:, None] + edge_shift[:, None]).astype(jnp.bfloat16)
    summed = column_scatter(message, receivers, cell_count)
    node_input = jnp.concatenate([node_state, summed.astype(jnp.bfloat16)], axis=0)
    node_linear = contract_first(node_first, node_input) + node_bias[:, None]
    node_active = sigmoid_linear(node_linear).astype(jnp.bfloat16)
    node_output = contract_first(node_second, node_active)
    node_scaled, node_spread = standardize(node_output)
    upstream = node_cotangent.astype(jnp.float32)
    node_delta, nodegain_delta, nodeshift_delta = normalize_back(
        upstream, node_scaled, node_spread, node_gain
    )
    node_delta = node_delta.astype(jnp.bfloat16)
    nodesecond_delta = contract_last(node_active, node_delta)
    node_hidden = jnp.dot(
        node_second, node_delta, preferred_element_type=jnp.float32
    ) * sigmoid_slope(node_linear)
    nodebias_delta = jnp.sum(node_hidden, axis=1)
    node_hidden = node_hidden.astype(jnp.bfloat16)
    nodefirst_delta = contract_last(node_input, node_hidden)
    node_back = jnp.dot(node_first, node_hidden, preferred_element_type=jnp.float32)
    message_delta = edge_cotangent.astype(jnp.float32) + column_gather(
        node_back[features:], receivers
    )
    edge_delta, edgegain_delta, edgeshift_delta = normalize_back(
        message_delta, edge_scaled, edge_spread, edge_gain
    )
    edge_delta = edge_delta.astype(jnp.bfloat16)
    edgesecond_delta = contract_last(edge_active, edge_delta)
    edge_hidden = jnp.dot(
        edge_second, edge_delta, preferred_element_type=jnp.float32
    ) * sigmoid_slope(edge_linear)
    edgebias_delta = jnp.sum(edge_hidden, axis=1)
    edge_hidden = edge_hidden.astype(jnp.bfloat16)
    edgefirst_delta = contract_last(stacked, edge_hidden)
    edge_back = jnp.dot(edge_first, edge_hidden, preferred_element_type=jnp.float32)
    edge_result = (edge_cotangent.astype(jnp.float32) + edge_back[2 * features :]).astype(
        jnp.bfloat16
    )
    scattered = column_scatter(edge_back[:features], senders, extended.shape[1])
    local_delta = (
        scattered[:, :cell_count]
        + column_scatter(edge_back[features : 2 * features], receivers, cell_count)
        + node_back[:features]
        + upstream
    )
    ghost_delta = scattered[:, cell_count:]
    partials = (
        edgefirst_delta,
        edgebias_delta,
        edgesecond_delta,
        edgegain_delta,
        edgeshift_delta,
        nodefirst_delta,
        nodebias_delta,
        nodesecond_delta,
        nodegain_delta,
        nodeshift_delta,
    )
    return (local_delta, ghost_delta, edge_result, partials)


def on_device(
    node_state,
    edge_state,
    senders,
    receivers,
    send_index,
    node_cotangent,
    edge_cotangent,
    edge_first,
    edge_bias,
    edge_second,
    edge_gain,
    edge_shift,
    node_first,
    node_bias,
    node_second,
    node_gain,
):
    features, cell_count = node_state.shape
    sub_count = lax.axis_size("sub")
    peer_count = 3 * sub_count
    halo_width = send_index.shape[2]
    index_rows = send_index.reshape(peer_count, halo_width)
    live_slots = index_rows >= 0
    safe_index = jnp.where(live_slots, index_rows, 0).reshape(-1)
    picked = column_gather(node_state, safe_index).reshape(features, peer_count, halo_width)
    outgoing = jnp.where(live_slots[None], picked, jnp.zeros_like(picked))
    blocks = outgoing.reshape(features, 3, sub_count, halo_width)
    across = lax.all_to_all(blocks, "sub", split_axis=2, concat_axis=2, tiled=True)
    upper = from_behind(across[:, 0], "dom", -1)
    lower = from_behind(across[:, 2], "dom", 1)
    ghost_rows = jnp.stack([upper, across[:, 1], lower], axis=1).reshape(
        features, peer_count, halo_width
    )
    extended = jnp.concatenate([node_state, ghost_rows.reshape(features, -1)], axis=1)
    local_delta, ghost_delta, edge_result, partials = local_backward(
        extended,
        node_state,
        edge_state,
        senders,
        receivers,
        node_cotangent,
        edge_cotangent,
        edge_first,
        edge_bias,
        edge_second,
        edge_gain,
        edge_shift,
        node_first,
        node_bias,
        node_second,
        node_gain,
    )
    ghost_delta = ghost_delta.reshape(features, peer_count, halo_width)
    grouped = ghost_delta.reshape(features, 3, sub_count, halo_width)
    further = from_behind(grouped[:, 0].astype(jnp.bfloat16), "dom", 1).astype(jnp.float32)
    nearer = from_behind(grouped[:, 2].astype(jnp.bfloat16), "dom", -1).astype(jnp.float32)
    regrouped = jnp.stack([further, grouped[:, 1], nearer], axis=1)
    returned = (
        lax.all_to_all(
            regrouped.astype(jnp.bfloat16), "sub", split_axis=2, concat_axis=2, tiled=True
        )
        .astype(regrouped.dtype)
        .reshape(features, peer_count, halo_width)
    )
    masked = jnp.where(live_slots[None], returned, jnp.zeros_like(returned)).reshape(features, -1)
    local_delta = local_delta + column_scatter(masked, safe_index, cell_count)
    totals = lax.psum(
        (
            partials[0],
            partials[1],
            partials[2],
            partials[3],
            partials[4],
            partials[5],
            partials[6],
            partials[7],
            partials[8],
            partials[9],
        ),
        ("dom", "sub"),
    )
    faces_total = edge_state.shape[1] * lax.axis_size("dom") * sub_count
    factor = 1.0 / math.sqrt(faces_total)
    (
        edgefirst_sum,
        edgebias_sum,
        edgesecond_sum,
        edgegain_sum,
        edgeshift_sum,
        nodefirst_sum,
        nodebias_sum,
        nodesecond_sum,
        nodegain_sum,
        nodeshift_sum,
    ) = totals
    return (
        local_delta.astype(jnp.bfloat16),
        edge_result,
        edgefirst_sum * factor,
        edgebias_sum * factor,
        edgesecond_sum * factor,
        edgegain_sum * factor,
        edgeshift_sum * factor,
        nodefirst_sum * factor,
        nodebias_sum * factor,
        nodesecond_sum * factor,
        nodegain_sum * factor,
        nodeshift_sum * factor,
    )


def solution(mesh):
    in_specs = (
        P(None, ("dom", "sub")),
        P(None, ("dom", "sub")),
        P(("dom", "sub")),
        P(("dom", "sub")),
        P(("dom", "sub"), None, None),
        P(None, ("dom", "sub")),
        P(None, ("dom", "sub")),
        P(),
        P(),
        P(),
        P(),
        P(),
        P(),
        P(),
        P(),
        P(),
    )
    out_specs = (
        P(None, ("dom", "sub")),
        P(None, ("dom", "sub")),
        P(),
        P(),
        P(),
        P(),
        P(),
        P(),
        P(),
        P(),
        P(),
        P(),
    )
    return jax.shard_map(
        on_device, mesh=mesh, in_specs=in_specs, out_specs=out_specs, check_vma=False
    )
```

profile of v0, /device:TPU:8, one launch (start us, length us, event | category | flops | bytes accessed | tf_op | source)
XLA Modules:
  0.0 289.5 jit_solution(8450819076300327334)
XLA Ops:
  8.7 4.2 %while.108 = (s32[]{:T(128)}, bf16[64,1536]{1,0:T(8,128)(2,1)S(1)}, s32[3,512]{1,0:T(4,128)S(1)}, bf16[64,1024]{1,0:T(8,128)(2,1)}, s32[]{:T(128)}, /*index=5*/s32[]{:T(128)}, s32[]{:T(128)}, s32[]{:T(128)}) while((s32[]{:T(128)}, bf16[64,1536]{1,0:T(8,128)(2,1)S(1)}, s32[3,512]{1,0:T(4,128)S(1)}, bf16[64,1024]{1,0:T(8,128)(2,1)}, s32[]{:T(128)}, ...), condition=%wide.region_1.2_spmd, body=%wide.region_0.1_spmd.sunk | while | flops 67665928 | bytes 202891 | solution.py:88
  13.8 3.4 %all-to-all-start = ((bf16[64,3,4,128]{3,0,1,2:T(8,128)(2,1)}), bf16[64,3,4,128]{3,0,1,2:T(8,128)(2,1)S(1)}, u32[]{:S(2)}, u32[]{:S(2)}) async-start(bf16[64,3,4,128]{3,0,1,2:T(8,128)(2,1)} %copy.47), calls=%async_computation | async-start | bytes 393216 | tf_op jit(solution)/shard_map/all_to_all | solution.py:227
  17.3 5.2 %all-to-all-done = bf16[64,3,4,128]{3,0,1,2:T(8,128)(2,1)S(1)} async-done(((bf16[64,3,4,128]{3,0,1,2:T(8,128)(2,1)}), bf16[64,3,4,128]{3,0,1,2:T(8,128)(2,1)S(1)}, u32[]{:S(2)}, u32[]{:S(2)}) %all-to-all-start) | async-done | bytes 196640 | tf_op jit(solution)/shard_map/all_to_all | solution.py:227
  22.5 3.4 %collective-permute-start.1 = (bf16[64,4,128]{2,0,1:T(8,128)(2,1)S(1)}, bf16[64,4,128]{2,0,1:T(8,128)(2,1)S(1)}, u32[]{:S(2)}, u32[]{:S(2)}) collective-permute-start(bf16[64,4,128]{2,0,1:T(8,128)(2,1)S(1)} %get-tuple-element.818), channel_id=1, source_target_pairs={{0,4},{4,8},{8,12},{12,16},{16,20},{20,24},{24,28},{1,5},{5,9},{9,... | collective-permute-start | bytes 196616 | tf_op jit(solution)/shard_map/ppermute | solution.py:13
  25.9 3.3 %collective-permute-start = (bf16[64,4,128]{2,0,1:T(8,128)(2,1)S(1)}, bf16[64,4,128]{2,0,1:T(8,128)(2,1)S(1)}, u32[]{:S(2)}, u32[]{:S(2)}) collective-permute-start(bf16[64,4,128]{2,0,1:T(8,128)(2,1)S(1)} %get-tuple-element.817), channel_id=1, source_target_pairs={{4,0},{8,4},{12,8},{16,12},{20,16},{24,20},{28,24},{5,1},{9,5},{13... | collective-permute-start | bytes 196616 | tf_op jit(solution)/shard_map/ppermute | solution.py:13
  29.3 3.0 %while.110 = (s32[]{:T(128)}, bf16[64,3072]{1,0:T(8,128)(2,1)S(1)}, s32[6,512]{1,0:T(8,128)S(1)}, bf16[64,1024]{1,0:T(8,128)(2,1)S(1)}, s32[]{:T(128)}, /*index=5*/s32[]{:T(128)}, s32[]{:T(128)}, s32[]{:T(128)}) while((s32[]{:T(128)}, bf16[64,3072]{1,0:T(8,128)(2,1)S(1)}, s32[6,512]{1,0:T(8,128)S(1)}, bf16[64,1024]{1,0:T(8,128)(2,1)S(1)}, ...), condition=%wide.region_5.6_spmd, body=%wide.region_4.5_spmd.sunk | while | flops 67665928 | bytes 202891 | solution.py:88
  32.8 11.0 %while.109 = (s32[]{:T(128)}, bf16[64,3072]{1,0:T(8,128)(2,1)S(1)}, s32[6,512]{1,0:T(8,128)S(1)}, bf16[64,1024]{1,0:T(8,128)(2,1)S(1)}, bf16[64,1536]{1,0:T(8,12...) while((s32[]{:T(128)}, bf16[64,3072]{1,0:T(8,128)(2,1)S(1)}, s32[6,512]{1,0:T(8,128)S(1)}, ...), condition=%wide.region_3.4_spmd, body=%wide.region_2.3_spmd.sunk | while | flops 169248768 | bytes 1472659 | solution.py:88
  47.2 3.7 %while.112 = (s32[]{:T(128)}, f32[64,1024]{1,0:T(8,128)S(1)}, bf16[64,3072]{1,0:T(8,128)(2,1)S(1)}, s32[6,512]{1,0:T(8,128)S(1)}, s32[]{:T(128)}, /*index=5*/s32[]{:T(128)}, s32[]{:T(128)}, s32[]{:T(128)}) while((s32[]{:T(128)}, f32[64,1024]{1,0:T(8,128)S(1)}, bf16[64,3072]{1,0:T(8,128)(2,1)S(1)}, s32[6,512]{1,0:T(8,128)S(1)}, ...), condition=%wide.region_9.10_spmd.clone, body=%wide.region_8.9_spmd.clone.sunk | while | flops 67764232 | bytes 596117 | solution.py:109
  56.0 11.1 %while.111 = (s32[]{:T(128)}, f32[64,3072]{1,0:T(8,128)S(1)}, s32[6,512]{1,0:T(8,128)S(1)}, f32[64,1024]{1,0:T(8,128)}, s32[]{:T(128)}, /*index=5*/s32[]{:T(128)}, s32[]{:T(128)}, s32[]{:T(128)}) while((s32[]{:T(128)}, f32[64,3072]{1,0:T(8,128)S(1)}, s32[6,512]{1,0:T(8,128)S(1)}, f32[64,1024]{1,0:T(8,128)}, s32[]{:T(128)}, ...), condition=%wide.region_15.16_spmd, body=%wide.region_14.15_spmd.sunk | while | flops 403177472 | bytes 399499 | solution.py:88
  56.1 1.8 fusion.184
  58.0 1.8 fusion.184
  59.8 1.8 fusion.184
  61.7 1.8 fusion.184
  63.5 1.8 fusion.184
  65.4 1.8 fusion.184
  73.9 45.6 %while.113 = (s32[]{:T(128)}, f32[64,2560]{1,0:T(8,128)S(1)}, f32[64,3072]{1,0:T(8,128)}, s32[6,512]{1,0:T(8,128)S(1)}, s32[]{:T(128)}, /*index=5*/s32[]{:T(128)}, s32[]{:T(128)}, s32[]{:T(128)}) while((s32[]{:T(128)}, f32[64,2560]{1,0:T(8,128)S(1)}, f32[64,3072]{1,0:T(8,128)}, s32[6,512]{1,0:T(8,128)S(1)}, s32[]{:T(128)}, ...), condition=%wide.region_19.20_spmd.clone, body=%wide.region_18.19_spmd.clone.sunk | while | flops 1008273408 | bytes 3307685 | solution.py:109
  73.9 1.5 convolution_dynamic-update-slice_fusion.10
  75.4 1.5 convolution_dynamic-update-slice_fusion.11
  81.5 1.5 convolution_dynamic-update-slice_fusion.10
  84.5 1.5 convolution_dynamic-update-slice_fusion.12
  89.1 1.5 convolution_dynamic-update-slice_fusion.10
  96.7 1.5 convolution_dynamic-update-slice_fusion.10
  104.3 1.5 convolution_dynamic-update-slice_fusion.10
  111.9 1.5 convolution_dynamic-update-slice_fusion.10
  119.7 4.0 %collective-permute-start.2 = (bf16[64,4,128]{2,1,0:T(4,128)(2,1)S(1)}, bf16[64,4,128]{2,1,0:T(4,128)(2,1)S(1)}, u32[]{:S(2)}, u32[]{:S(2)}) collective-permute-start(bf16[64,4,128]{2,1,0:T(4,128)(2,1)S(1)} %get-tuple-element.814), channel_id=1, source_target_pairs={{0,4},{4,8},{8,12},{12,16},{16,20},{20,24},{24,28},{1,5},{5,9},{9,... | collective-permute-start | bytes 196616 | tf_op jit(solution)/shard_map/ppermute | solution.py:13
  123.6 2.9 %collective-permute-start.3 = (bf16[64,4,128]{2,1,0:T(4,128)(2,1)S(1)}, bf16[64,4,128]{2,1,0:T(4,128)(2,1)S(1)}, u32[]{:S(2)}, u32[]{:S(2)}) collective-permute-start(bf16[64,4,128]{2,1,0:T(4,128)(2,1)S(1)} %get-tuple-element.815), channel_id=1, source_target_pairs={{4,0},{8,4},{12,8},{16,12},{20,16},{24,20},{28,24},{5,1},{9,5},{13... | collective-permute-start | bytes 196616 | tf_op jit(solution)/shard_map/ppermute | solution.py:13
  126.6 6.2 %while.114 = (s32[]{:T(128)}, f32[64,1024]{1,0:T(8,128)S(1)}, f32[64,3072]{1,0:T(8,128)S(1)}, s32[6,512]{1,0:T(8,128)S(1)}, s32[]{:T(128)}, /*index=5*/s32[]{:T(128)}, s32[]{:T(128)}, s32[]{:T(128)}) while((s32[]{:T(128)}, f32[64,1024]{1,0:T(8,128)S(1)}, f32[64,3072]{1,0:T(8,128)S(1)}, s32[6,512]{1,0:T(8,128)S(1)}, s32[]{:T(128)}, ...), condition=%wide.region_21.22_spmd.clone, body=%wide.region_20.21_spmd.clone.sunk | while | flops 403308544 | bytes 661653 | solution.py:109
  132.9 124.7 %all-reduce.3.cloned.1.call-done = (f32[192,64]{0,1:T(8,128)}, f32[64]{0:T(128)}, f32[64,64]{1,0:T(8,128)}, f32[64]{0:T(128)}, f32[64]{0:T(128)}, /*index=5*/f32...) async-done(((f32[192,64]{0,1:T(8,128)}, f32[64]{0:T(128)}, f32[64,64]{1,0:T(8,128)}, f32[64]{0:T(128)}, f32[64]{0:T(128)}, ...) | async-done | bytes 116240 | tf_op jit(solution)/shard_map/psum | solution.py:266
  257.6 1.5 broadcast_multiply_fusion
  269.8 3.4 %all-to-all-start.1 = ((bf16[64,3,4,128]{3,0,1,2:T(8,128)(2,1)}), bf16[64,3,4,128]{3,0,1,2:T(8,128)(2,1)S(1)}, u32[]{:S(2)}, u32[]{:S(2)}) async-start(bf16[64,3,4,128]{3,0,1,2:T(8,128)(2,1)} %copy.54), calls=%async_computation.1 | async-start | bytes 393216 | tf_op jit(solution)/shard_map/all_to_all | solution.py:258
  274.3 4.1 %all-to-all-done.1 = bf16[64,3,4,128]{3,0,1,2:T(8,128)(2,1)S(1)} async-done(((bf16[64,3,4,128]{3,0,1,2:T(8,128)(2,1)}), bf16[64,3,4,128]{3,0,1,2:T(8,128)(2,1)S(1)}, u32[]{:S(2)}, u32[]{:S(2)}) %all-to-all-start.1) | async-done | bytes 196640 | tf_op jit(solution)/shard_map/all_to_all | solution.py:258
  278.8 3.1 %while.115 = (s32[]{:T(128)}, f32[64,1024]{1,0:T(8,128)S(1)}, f32[64,1536]{1,0:T(8,128)S(1)}, s32[3,512]{1,0:T(4,128)S(1)}, s32[]{:T(128)}, /*index=5*/s32[]{:T(128)}, s32[]{:T(128)}, s32[]{:T(128)}) while((s32[]{:T(128)}, f32[64,1024]{1,0:T(8,128)S(1)}, f32[64,1536]{1,0:T(8,128)S(1)}, s32[3,512]{1,0:T(4,128)S(1)}, s32[]{:T(128)}, ...), condition=%wide.region_23.24_spmd.clone, body=%wide.region_22.23_spmd.clone.sunk | while | flops 403308544 | bytes 661653 | solution.py:109
  (294 shorter events, 94.2 us)
Async XLA Ops:
  7.2 36.8 %copy-start = (bf16[192,64]{0,1:T(8,128)(2,1)S(1)}, bf16[192,64]{0,1:T(8,128)(2,1)}, u32[]{:S(2)}) copy-start(bf16[192,64]{0,1:T(8,128)(2,1)} %param.39) | copy-start | bytes 73732
  8.7 8.6 %copy-start.13 = (s32[3072]{0:T(1024)S(1)}, s32[3072]{0:T(1024)}, u32[]{:S(2)}) copy-start(s32[3072]{0:T(1024)} %param.35) | copy-start | bytes 36868
  12.9 16.3 %copy-start.18 = (bf16[64,1024]{1,0:T(8,128)(2,1)S(1)}, bf16[64,1024]{1,0:T(8,128)(2,1)}, u32[]{:S(2)}) copy-start(bf16[64,1024]{1,0:T(8,128)(2,1)} %get-tuple-element.1290) | copy-start | bytes 393220
  13.8 8.6 %all-to-all-start = ((bf16[64,3,4,128]{3,0,1,2:T(8,128)(2,1)}), bf16[64,3,4,128]{3,0,1,2:T(8,128)(2,1)S(1)}, u32[]{:S(2)}, u32[]{:S(2)}) async-start(bf16[64,3,4,128]{3,0,1,2:T(8,128)(2,1)} %copy.47), calls=%async_computation | async-start | bytes 393216 | tf_op jit(solution)/shard_map/all_to_all | solution.py:227
  17.2 240.4 %all-reduce.3.cloned.1.call-start = ((), (), s32[]{:S(2)}) async-start(), calls=%async_computation.2 | async-start | bytes 333824 | tf_op jit(solution)/shard_map/psum | solution.py:266
  22.5 9.9 %collective-permute-start.1 = (bf16[64,4,128]{2,0,1:T(8,128)(2,1)S(1)}, bf16[64,4,128]{2,0,1:T(8,128)(2,1)S(1)}, u32[]{:S(2)}, u32[]{:S(2)}) collective-permute-start(bf16[64,4,128]{2,0,1:T(8,128)(2,1)S(1)} %get-tuple-element.818), channel_id=1, source_target_pairs={{0,4},{4,8},{8,12},{12,16},{16,20},{20,24},{24,28},{1,5},{5,9},{9,... | collective-permute-start | bytes 196616 | tf_op jit(solution)/shard_map/ppermute | solution.py:13
  25.9 6.5 %collective-permute-start = (bf16[64,4,128]{2,0,1:T(8,128)(2,1)S(1)}, bf16[64,4,128]{2,0,1:T(8,128)(2,1)S(1)}, u32[]{:S(2)}, u32[]{:S(2)}) collective-permute-start(bf16[64,4,128]{2,0,1:T(8,128)(2,1)S(1)} %get-tuple-element.817), channel_id=1, source_target_pairs={{4,0},{8,4},{12,8},{16,12},{20,16},{24,20},{28,24},{5,1},{9,5},{13... | collective-permute-start | bytes 196616 | tf_op jit(solution)/shard_map/ppermute | solution.py:13
  29.3 3.1 %copy-start.14 = (s32[3072]{0:T(1024)S(1)}, s32[3072]{0:T(1024)}, u32[]{:S(2)}) copy-start(s32[3072]{0:T(1024)} %param.34) | copy-start | bytes 36868
  32.8 11.1 %copy-start.7 = (bf16[64,3072]{1,0:T(8,128)(2,1)S(1)}, bf16[64,3072]{1,0:T(8,128)(2,1)}, u32[]{:S(2)}) copy-start(bf16[64,3072]{1,0:T(8,128)(2,1)} %param.33) | copy-start | bytes 1179652
  43.8 0.7 copy-start.19
  44.5 1.3 copy-start.2
  44.5 2.0 copy-start.10
  44.5 2.5 copy-start.15
  44.5 2.5 copy-start.17
  45.8 0.7 copy-start.4
  47.2 3.8 %copy-start.12 = (bf16[128,64]{0,1:T(8,128)(2,1)S(1)}, bf16[128,64]{0,1:T(8,128)(2,1)}, u32[]{:S(2)}) copy-start(bf16[128,64]{0,1:T(8,128)(2,1)} %param.44) | copy-start | bytes 49156
  47.2 3.8 %copy-start.20 = (f32[64]{0:T(128)S(1)}, f32[64]{0:T(128)}, u32[]{:S(2)}) copy-start(f32[64]{0:T(128)} %param.45) | copy-start | bytes 772
  47.2 4.0 %copy-start.11 = (bf16[64,64]{1,0:T(8,128)(2,1)S(1)}, bf16[64,64]{1,0:T(8,128)(2,1)}, u32[]{:S(2)}) copy-start(bf16[64,64]{1,0:T(8,128)(2,1)} %param.46) | copy-start | bytes 24580
  50.9 0.9 copy-start.6
  50.9 0.9 copy-start.16
  56.0 11.2 %copy-start.1 = (bf16[64,3072]{1,0:T(8,128)(2,1)S(1)}, bf16[64,3072]{1,0:T(8,128)(2,1)}, u32[]{:S(2)}) copy-start(bf16[64,3072]{1,0:T(8,128)(2,1)} %param.38) | copy-start | bytes 1179652
  67.2 1.7 copy-start.5
  68.6 1.2 copy-start.21
  69.7 1.3 copy-start.3
  73.8 52.8 %copy-start.9 = (f32[64,1024]{1,0:T(8,128)S(1)}, f32[64,1024]{1,0:T(8,128)}, u32[]{:S(2)}) copy-start(f32[64,1024]{1,0:T(8,128)} %custom-call.2) | copy-start | bytes 786436
  119.7 149.3 %collective-permute-start.2 = (bf16[64,4,128]{2,1,0:T(4,128)(2,1)S(1)}, bf16[64,4,128]{2,1,0:T(4,128)(2,1)S(1)}, u32[]{:S(2)}, u32[]{:S(2)}) collective-permute-start(bf16[64,4,128]{2,1,0:T(4,128)(2,1)S(1)} %get-tuple-element.814), channel_id=1, source_target_pairs={{0,4},{4,8},{8,12},{12,16},{16,20},{20,24},{24,28},{1,5},{5,9},{9,... | collective-permute-start | bytes 196616 | tf_op jit(solution)/shard_map/ppermute | solution.py:13
  123.6 145.3 %collective-permute-start.3 = (bf16[64,4,128]{2,1,0:T(4,128)(2,1)S(1)}, bf16[64,4,128]{2,1,0:T(4,128)(2,1)S(1)}, u32[]{:S(2)}, u32[]{:S(2)}) collective-permute-start(bf16[64,4,128]{2,1,0:T(4,128)(2,1)S(1)} %get-tuple-element.815), channel_id=1, source_target_pairs={{4,0},{8,4},{12,8},{16,12},{20,16},{24,20},{28,24},{5,1},{9,5},{13... | collective-permute-start | bytes 196616 | tf_op jit(solution)/shard_map/ppermute | solution.py:13
  132.9 145.9 %copy-start.8 = (f32[64,1024]{1,0:T(8,128)S(1)}, f32[64,1024]{1,0:T(8,128)}, u32[]{:S(2)}) copy-start(f32[64,1024]{1,0:T(8,128)} %custom-call.3) | copy-start | bytes 786436
  269.8 8.6 %all-to-all-start.1 = ((bf16[64,3,4,128]{3,0,1,2:T(8,128)(2,1)}), bf16[64,3,4,128]{3,0,1,2:T(8,128)(2,1)S(1)}, u32[]{:S(2)}, u32[]{:S(2)}) async-start(bf16[64,3,4,128]{3,0,1,2:T(8,128)(2,1)} %copy.54), calls=%async_computation.1 | async-start | bytes 393216 | tf_op jit(solution)/shard_map/all_to_all | solution.py:258
Sparse Core Ops, SparseCore 0:
  126.7 130.8 all-reduce.2
where the time goes:
time: 291 us; the launch traced here: 289 us
  waiting for transfers between devices  134 us (46%)
  matrix products  92.7 us (32%)
  starting transfers between devices  20.4 us (7%)
  other arithmetic  20.3 us (7%)
  between operations  14.7 us (5%)
  local copies, waits for them, and re-layouts  5.33 us (2%)
    psum x1, waiting for transfers between devices, on_device(): lax.psum((partials[0], partials[1], partials[2], partials[3], partials[4]...  125 us
    dot_general x45, matrix products, one_block(): jnp.dot(portion, selector, precision=precision, preferred_element_type=jn...  56.2 us
    dot_general x45, matrix products, one_block(): jnp.dot(table[:, begin:begin + piece], selector, precision=precision, pre...  28.1 us
    ppermute x4, starting transfers between devices, from_behind(): lax.ppermute(value, axis, [(source, source + steps) for source in range(f...  13.7 us
  transfers between devices with their start and end apart: 7, of which 3 were waited for; matrix products, arithmetic and copies ran while one was open for 7% of the time, Pallas kernels for 0%

commit v1 on v0

--- a/solution.py
+++ b/solution.py
@@ -3,6 +3,7 @@
 import jax.numpy as jnp
 from jax import lax
 from jax.sharding import PartitionSpec as P
+from jax.lax import psum
 
 EPSILON = 1e-05
 
@@ -263,20 +264,23 @@
     )
     masked = jnp.where(live_slots[None], returned, jnp.zeros_like(returned)).reshape(features, -1)
     local_delta = local_delta + column_scatter(masked, safe_index, cell_count)
-    totals = lax.psum(
-        (
-            partials[0],
-            partials[1],
-            partials[2],
-            partials[3],
-            partials[4],
-            partials[5],
-            partials[6],
-            partials[7],
-            partials[8],
-            partials[9],
+    totals = psum(
+        psum(
+            (
+                partials[0],
+                partials[1],
+                partials[2],
+                partials[3],
+                partials[4],
+                partials[5],
+                partials[6],
+                partials[7],
+                partials[8],
+                partials[9],
+            ),
+            "dom",
         ),
-        ("dom", "sub"),
+        "sub",
     )
     faces_total = edge_state.shape[1] * lax.axis_size("dom") * sub_count
     factor = 1.0 / math.sqrt(faces_total)

time: 291 us -> 260 us (0.89)
  waiting for transfers between devices: 134 us -> 101 us
    psum x1 -> x2, waiting for transfers between devices: 125 us -> 96.2 us  [the longest x1 65.9 us: on_device(): psum((partials[0], partials[1], partials[2], partials[3], partials[4], pa...]
    all_to_all x1, waiting for transfers between devices: 4.15 us -> 0.01 us  [on_device(): lax.all_to_all(regrouped.astype(jnp.bfloat16), 'sub', split_axis=2, conca...]
  transfers between devices with their start and end apart: 7 -> 8, of which waited for: 3 -> 3; matrix products, arithmetic and copies ran while one was open for 7% -> 9% of each run, Pallas kernels for 0% -> 0%
where the time goes in v1:
time: 260 us; the launch traced here: 257 us
  waiting for transfers between devices  101 us (39%)
  matrix products  92.7 us (36%)
  starting transfers between devices  20.5 us (8%)
  other arithmetic  20.2 us (8%)
  between operations  14.7 us (6%)
  local copies, waits for them, and re-layouts  5.32 us (2%)
    psum x1, waiting for transfers between devices, on_device(): psum((partials[0], partials[1], partials[2], partials[3], partials[4], pa...  65.9 us
    dot_general x45, matrix products, one_block(): jnp.dot(portion, selector, precision=precision, preferred_element_type=jn...  56.2 us
    psum x1, waiting for transfers between devices, on_device(): psum(psum((partials[0], partials[1], partials[2], partials[3], partials[4...  30.3 us
    dot_general x45, matrix products, one_block(): jnp.dot(table[:, begin:begin + piece], selector, precision=precision, pre...  28.1 us
    ppermute x4, starting transfers between devices, from_behind(): lax.ppermute(value, axis, [(source, source + steps) for source in range(f...  13.5 us
  transfers between devices with their start and end apart: 8, of which 3 were waited for; matrix products, arithmetic and copies ran while one was open for 9% of the time, Pallas kernels for 0%

profile of v1, /device:TPU:8, one launch (start us, length us, event | category | flops | bytes accessed | tf_op | source)
XLA Modules:
  0.0 256.9 jit_solution(16681501918363239823)
XLA Ops:
  8.7 4.2 %while.108 = (s32[]{:T(128)}, bf16[64,1536]{1,0:T(8,128)(2,1)S(1)}, s32[3,512]{1,0:T(4,128)S(1)}, bf16[64,1024]{1,0:T(8,128)(2,1)}, s32[]{:T(128)}, /*index=5*/s32[]{:T(128)}, s32[]{:T(128)}, s32[]{:T(128)}) while((s32[]{:T(128)}, bf16[64,1536]{1,0:T(8,128)(2,1)S(1)}, s32[3,512]{1,0:T(4,128)S(1)}, bf16[64,1024]{1,0:T(8,128)(2,1)}, s32[]{:T(128)}, ...), condition=%wide.region_1.2_spmd, body=%wide.region_0.1_spmd.sunk | while | flops 67665928 | bytes 202891 | solution.py:89
  13.8 3.4 %all-to-all-start = ((bf16[64,3,4,128]{3,0,1,2:T(8,128)(2,1)}), bf16[64,3,4,128]{3,0,1,2:T(8,128)(2,1)S(1)}, u32[]{:S(2)}, u32[]{:S(2)}) async-start(bf16[64,3,4,128]{3,0,1,2:T(8,128)(2,1)} %copy.47), calls=%async_computation | async-start | bytes 393216 | tf_op jit(solution)/shard_map/all_to_all | solution.py:228
  17.3 5.2 %all-to-all-done = bf16[64,3,4,128]{3,0,1,2:T(8,128)(2,1)S(1)} async-done(((bf16[64,3,4,128]{3,0,1,2:T(8,128)(2,1)}), bf16[64,3,4,128]{3,0,1,2:T(8,128)(2,1)S(1)}, u32[]{:S(2)}, u32[]{:S(2)}) %all-to-all-start) | async-done | bytes 196640 | tf_op jit(solution)/shard_map/all_to_all | solution.py:228
  22.5 3.4 %collective-permute-start.1 = (bf16[64,4,128]{2,0,1:T(8,128)(2,1)S(1)}, bf16[64,4,128]{2,0,1:T(8,128)(2,1)S(1)}, u32[]{:S(2)}, u32[]{:S(2)}) collective-permute-start(bf16[64,4,128]{2,0,1:T(8,128)(2,1)S(1)} %get-tuple-element.828), channel_id=1, source_target_pairs={{0,4},{4,8},{8,12},{12,16},{16,20},{20,24},{24,28},{1,5},{5,9},{9,... | collective-permute-start | bytes 196616 | tf_op jit(solution)/shard_map/ppermute | solution.py:14
  25.9 3.3 %collective-permute-start = (bf16[64,4,128]{2,0,1:T(8,128)(2,1)S(1)}, bf16[64,4,128]{2,0,1:T(8,128)(2,1)S(1)}, u32[]{:S(2)}, u32[]{:S(2)}) collective-permute-start(bf16[64,4,128]{2,0,1:T(8,128)(2,1)S(1)} %get-tuple-element.827), channel_id=1, source_target_pairs={{4,0},{8,4},{12,8},{16,12},{20,16},{24,20},{28,24},{5,1},{9,5},{13... | collective-permute-start | bytes 196616 | tf_op jit(solution)/shard_map/ppermute | solution.py:14
  29.3 3.0 %while.110 = (s32[]{:T(128)}, bf16[64,3072]{1,0:T(8,128)(2,1)S(1)}, s32[6,512]{1,0:T(8,128)S(1)}, bf16[64,1024]{1,0:T(8,128)(2,1)S(1)}, s32[]{:T(128)}, /*index=5*/s32[]{:T(128)}, s32[]{:T(128)}, s32[]{:T(128)}) while((s32[]{:T(128)}, bf16[64,3072]{1,0:T(8,128)(2,1)S(1)}, s32[6,512]{1,0:T(8,128)S(1)}, bf16[64,1024]{1,0:T(8,128)(2,1)S(1)}, ...), condition=%wide.region_5.6_spmd, body=%wide.region_4.5_spmd.sunk | while | flops 67665928 | bytes 202891 | solution.py:89
  32.8 11.0 %while.109 = (s32[]{:T(128)}, bf16[64,3072]{1,0:T(8,128)(2,1)S(1)}, s32[6,512]{1,0:T(8,128)S(1)}, bf16[64,1024]{1,0:T(8,128)(2,1)S(1)}, bf16[64,1536]{1,0:T(8,12...) while((s32[]{:T(128)}, bf16[64,3072]{1,0:T(8,128)(2,1)S(1)}, s32[6,512]{1,0:T(8,128)S(1)}, ...), condition=%wide.region_3.4_spmd, body=%wide.region_2.3_spmd.sunk | while | flops 169248768 | bytes 1472659 | solution.py:89
  47.2 3.7 %while.112 = (s32[]{:T(128)}, f32[64,1024]{1,0:T(8,128)S(1)}, bf16[64,3072]{1,0:T(8,128)(2,1)S(1)}, s32[6,512]{1,0:T(8,128)S(1)}, s32[]{:T(128)}, /*index=5*/s32[]{:T(128)}, s32[]{:T(128)}, s32[]{:T(128)}) while((s32[]{:T(128)}, f32[64,1024]{1,0:T(8,128)S(1)}, bf16[64,3072]{1,0:T(8,128)(2,1)S(1)}, s32[6,512]{1,0:T(8,128)S(1)}, ...), condition=%wide.region_9.10_spmd.clone, body=%wide.region_8.9_spmd.clone.sunk | while | flops 67764232 | bytes 596117 | solution.py:110
  56.1 11.1 %while.111 = (s32[]{:T(128)}, f32[64,3072]{1,0:T(8,128)S(1)}, s32[6,512]{1,0:T(8,128)S(1)}, f32[64,1024]{1,0:T(8,128)}, s32[]{:T(128)}, /*index=5*/s32[]{:T(128)}, s32[]{:T(128)}, s32[]{:T(128)}) while((s32[]{:T(128)}, f32[64,3072]{1,0:T(8,128)S(1)}, s32[6,512]{1,0:T(8,128)S(1)}, f32[64,1024]{1,0:T(8,128)}, s32[]{:T(128)}, ...), condition=%wide.region_15.16_spmd, body=%wide.region_14.15_spmd.sunk | while | flops 403177472 | bytes 399499 | solution.py:89
  56.1 1.8 fusion.184
  58.0 1.8 fusion.184
  59.9 1.8 fusion.184
  61.7 1.8 fusion.184
  63.6 1.8 fusion.184
  65.4 1.8 fusion.184
  73.9 45.6 %while.113 = (s32[]{:T(128)}, f32[64,2560]{1,0:T(8,128)S(1)}, f32[64,3072]{1,0:T(8,128)}, s32[6,512]{1,0:T(8,128)S(1)}, s32[]{:T(128)}, /*index=5*/s32[]{:T(128)}, s32[]{:T(128)}, s32[]{:T(128)}) while((s32[]{:T(128)}, f32[64,2560]{1,0:T(8,128)S(1)}, f32[64,3072]{1,0:T(8,128)}, s32[6,512]{1,0:T(8,128)S(1)}, s32[]{:T(128)}, ...), condition=%wide.region_19.20_spmd.clone, body=%wide.region_18.19_spmd.clone.sunk | while | flops 1008273408 | bytes 3307685 | solution.py:110
  73.9 1.5 convolution_dynamic-update-slice_fusion.10
  75.4 1.5 convolution_dynamic-update-slice_fusion.11
  81.5 1.5 convolution_dynamic-update-slice_fusion.10
  87.4 1.5 convolution_dynamic-update-slice_fusion.14
  89.1 1.5 convolution_dynamic-update-slice_fusion.10
  96.8 1.5 convolution_dynamic-update-slice_fusion.10
  104.4 1.5 convolution_dynamic-update-slice_fusion.10
  112.0 1.5 convolution_dynamic-update-slice_fusion.10
  119.7 4.0 %collective-permute-start.2 = (bf16[64,4,128]{2,1,0:T(4,128)(2,1)S(1)}, bf16[64,4,128]{2,1,0:T(4,128)(2,1)S(1)}, u32[]{:S(2)}, u32[]{:S(2)}) collective-permute-start(bf16[64,4,128]{2,1,0:T(4,128)(2,1)S(1)} %get-tuple-element.824), channel_id=1, source_target_pairs={{0,4},{4,8},{8,12},{12,16},{16,20},{20,24},{24,28},{1,5},{5,9},{9,... | collective-permute-start | bytes 196616 | tf_op jit(solution)/shard_map/ppermute | solution.py:14
  123.7 2.8 %collective-permute-start.3 = (bf16[64,4,128]{2,1,0:T(4,128)(2,1)S(1)}, bf16[64,4,128]{2,1,0:T(4,128)(2,1)S(1)}, u32[]{:S(2)}, u32[]{:S(2)}) collective-permute-start(bf16[64,4,128]{2,1,0:T(4,128)(2,1)S(1)} %get-tuple-element.825), channel_id=1, source_target_pairs={{4,0},{8,4},{12,8},{16,12},{20,16},{24,20},{28,24},{5,1},{9,5},{13... | collective-permute-start | bytes 196616 | tf_op jit(solution)/shard_map/ppermute | solution.py:14
  126.7 6.2 %while.114 = (s32[]{:T(128)}, f32[64,1024]{1,0:T(8,128)S(1)}, f32[64,3072]{1,0:T(8,128)S(1)}, s32[6,512]{1,0:T(8,128)S(1)}, s32[]{:T(128)}, /*index=5*/s32[]{:T(128)}, s32[]{:T(128)}, s32[]{:T(128)}) while((s32[]{:T(128)}, f32[64,1024]{1,0:T(8,128)S(1)}, f32[64,3072]{1,0:T(8,128)S(1)}, s32[6,512]{1,0:T(8,128)S(1)}, s32[]{:T(128)}, ...), condition=%wide.region_21.22_spmd.clone, body=%wide.region_20.21_spmd.clone.sunk | while | flops 403308544 | bytes 661653 | solution.py:110
  133.0 65.9 %all-reduce.5.cloned.1.call-done = (f32[192,64]{0,1:T(8,128)}, f32[64]{0:T(128)}, f32[64,64]{1,0:T(8,128)}, f32[64]{0:T(128)}, f32[64]{0:T(128)}, /*index=5*/f32...) async-done(((f32[192,64]{0,1:T(8,128)}, f32[64]{0:T(128)}, f32[64,64]{1,0:T(8,128)}, f32[64]{0:T(128)}, f32[64]{0:T(128)}, ...) | async-done | bytes 116240 | tf_op jit(solution)/shard_map/psum | solution.py:268
  199.8 3.4 %all-to-all-start.1 = ((bf16[64,3,4,128]{3,0,1,2:T(8,128)(2,1)}), bf16[64,3,4,128]{3,0,1,2:T(8,128)(2,1)S(1)}, u32[]{:S(2)}, u32[]{:S(2)}) async-start(bf16[64,3,4,128]{3,0,1,2:T(8,128)(2,1)} %copy.54), calls=%async_computation.1 | async-start | bytes 393216 | tf_op jit(solution)/shard_map/all_to_all | solution.py:259
  203.2 30.3 %all-reduce.7.cloned.1.call-done = (f32[192,64]{0,1:T(8,128)}, f32[64]{0:T(128)}, f32[64,64]{1,0:T(8,128)}, f32[64]{0:T(128)}, f32[64]{0:T(128)}, /*index=5*/f32...) async-done(((f32[192,64]{0,1:T(8,128)}, f32[64]{0:T(128)}, f32[64,64]{1,0:T(8,128)}, f32[64]{0:T(128)}, f32[64]{0:T(128)}, ...) | async-done | bytes 116240 | tf_op jit(solution)/shard_map/psum | solution.py:267
  233.5 1.5 broadcast_multiply_fusion
  246.2 3.1 %while.115 = (s32[]{:T(128)}, f32[64,1024]{1,0:T(8,128)S(1)}, f32[64,1536]{1,0:T(8,128)S(1)}, s32[3,512]{1,0:T(4,128)S(1)}, s32[]{:T(128)}, /*index=5*/s32[]{:T(128)}, s32[]{:T(128)}, s32[]{:T(128)}) while((s32[]{:T(128)}, f32[64,1024]{1,0:T(8,128)S(1)}, f32[64,1536]{1,0:T(8,128)S(1)}, s32[3,512]{1,0:T(4,128)S(1)}, s32[]{:T(128)}, ...), condition=%wide.region_23.24_spmd.clone, body=%wide.region_22.23_spmd.clone.sunk | while | flops 403308544 | bytes 661653 | solution.py:110
  (297 shorter events, 94.4 us)
Async XLA Ops:
  7.2 36.8 %copy-start = (bf16[192,64]{0,1:T(8,128)(2,1)S(1)}, bf16[192,64]{0,1:T(8,128)(2,1)}, u32[]{:S(2)}) copy-start(bf16[192,64]{0,1:T(8,128)(2,1)} %param.39) | copy-start | bytes 73732
  8.7 8.6 %copy-start.13 = (s32[3072]{0:T(1024)S(1)}, s32[3072]{0:T(1024)}, u32[]{:S(2)}) copy-start(s32[3072]{0:T(1024)} %param.35) | copy-start | bytes 36868
  12.9 16.3 %copy-start.18 = (bf16[64,1024]{1,0:T(8,128)(2,1)S(1)}, bf16[64,1024]{1,0:T(8,128)(2,1)}, u32[]{:S(2)}) copy-start(bf16[64,1024]{1,0:T(8,128)(2,1)} %get-tuple-element.1342) | copy-start | bytes 393220
  13.8 8.6 %all-to-all-start = ((bf16[64,3,4,128]{3,0,1,2:T(8,128)(2,1)}), bf16[64,3,4,128]{3,0,1,2:T(8,128)(2,1)S(1)}, u32[]{:S(2)}, u32[]{:S(2)}) async-start(bf16[64,3,4,128]{3,0,1,2:T(8,128)(2,1)} %copy.47), calls=%async_computation | async-start | bytes 393216 | tf_op jit(solution)/shard_map/all_to_all | solution.py:228
  17.2 181.7 %all-reduce.5.cloned.1.call-start = ((), (), s32[]{:S(2)}) async-start(), calls=%async_computation.2 | async-start | bytes 333824 | tf_op jit(solution)/shard_map/psum | solution.py:268
  22.5 9.9 %collective-permute-start.1 = (bf16[64,4,128]{2,0,1:T(8,128)(2,1)S(1)}, bf16[64,4,128]{2,0,1:T(8,128)(2,1)S(1)}, u32[]{:S(2)}, u32[]{:S(2)}) collective-permute-start(bf16[64,4,128]{2,0,1:T(8,128)(2,1)S(1)} %get-tuple-element.828), channel_id=1, source_target_pairs={{0,4},{4,8},{8,12},{12,16},{16,20},{20,24},{24,28},{1,5},{5,9},{9,... | collective-permute-start | bytes 196616 | tf_op jit(solution)/shard_map/ppermute | solution.py:14
  25.9 6.5 %collective-permute-start = (bf16[64,4,128]{2,0,1:T(8,128)(2,1)S(1)}, bf16[64,4,128]{2,0,1:T(8,128)(2,1)S(1)}, u32[]{:S(2)}, u32[]{:S(2)}) collective-permute-start(bf16[64,4,128]{2,0,1:T(8,128)(2,1)S(1)} %get-tuple-element.827), channel_id=1, source_target_pairs={{4,0},{8,4},{12,8},{16,12},{20,16},{24,20},{28,24},{5,1},{9,5},{13... | collective-permute-start | bytes 196616 | tf_op jit(solution)/shard_map/ppermute | solution.py:14
  29.3 3.1 %copy-start.14 = (s32[3072]{0:T(1024)S(1)}, s32[3072]{0:T(1024)}, u32[]{:S(2)}) copy-start(s32[3072]{0:T(1024)} %param.34) | copy-start | bytes 36868
  32.8 11.1 %copy-start.7 = (bf16[64,3072]{1,0:T(8,128)(2,1)S(1)}, bf16[64,3072]{1,0:T(8,128)(2,1)}, u32[]{:S(2)}) copy-start(bf16[64,3072]{1,0:T(8,128)(2,1)} %param.33) | copy-start | bytes 1179652
  43.8 0.7 copy-start.19
  44.5 1.3 copy-start.2
  44.5 2.1 copy-start.10
  44.5 2.5 copy-start.15
  44.5 2.5 copy-start.17
  45.8 0.7 copy-start.4
  47.2 3.8 %copy-start.12 = (bf16[128,64]{0,1:T(8,128)(2,1)S(1)}, bf16[128,64]{0,1:T(8,128)(2,1)}, u32[]{:S(2)}) copy-start(bf16[128,64]{0,1:T(8,128)(2,1)} %param.44) | copy-start | bytes 49156
  47.2 3.8 %copy-start.20 = (f32[64]{0:T(128)S(1)}, f32[64]{0:T(128)}, u32[]{:S(2)}) copy-start(f32[64]{0:T(128)} %param.45) | copy-start | bytes 772
  47.2 4.0 %copy-start.11 = (bf16[64,64]{1,0:T(8,128)(2,1)S(1)}, bf16[64,64]{1,0:T(8,128)(2,1)}, u32[]{:S(2)}) copy-start(bf16[64,64]{1,0:T(8,128)(2,1)} %param.46) | copy-start | bytes 24580
  50.9 0.9 copy-start.6
  50.9 0.9 copy-start.16
  56.1 11.2 %copy-start.1 = (bf16[64,3072]{1,0:T(8,128)(2,1)S(1)}, bf16[64,3072]{1,0:T(8,128)(2,1)}, u32[]{:S(2)}) copy-start(bf16[64,3072]{1,0:T(8,128)(2,1)} %param.38) | copy-start | bytes 1179652
  67.2 1.7 copy-start.5
  68.6 1.2 copy-start.21
  69.8 1.3 copy-start.3
  73.9 52.8 %copy-start.9 = (f32[64,1024]{1,0:T(8,128)S(1)}, f32[64,1024]{1,0:T(8,128)}, u32[]{:S(2)}) copy-start(f32[64,1024]{1,0:T(8,128)} %custom-call.2) | copy-start | bytes 786436
  119.7 79.2 %collective-permute-start.2 = (bf16[64,4,128]{2,1,0:T(4,128)(2,1)S(1)}, bf16[64,4,128]{2,1,0:T(4,128)(2,1)S(1)}, u32[]{:S(2)}, u32[]{:S(2)}) collective-permute-start(bf16[64,4,128]{2,1,0:T(4,128)(2,1)S(1)} %get-tuple-element.824), channel_id=1, source_target_pairs={{0,4},{4,8},{8,12},{12,16},{16,20},{20,24},{24,28},{1,5},{5,9},{9,... | collective-permute-start | bytes 196616 | tf_op jit(solution)/shard_map/ppermute | solution.py:14
  123.7 75.2 %collective-permute-start.3 = (bf16[64,4,128]{2,1,0:T(4,128)(2,1)S(1)}, bf16[64,4,128]{2,1,0:T(4,128)(2,1)S(1)}, u32[]{:S(2)}, u32[]{:S(2)}) collective-permute-start(bf16[64,4,128]{2,1,0:T(4,128)(2,1)S(1)} %get-tuple-element.825), channel_id=1, source_target_pairs={{4,0},{8,4},{12,8},{16,12},{20,16},{24,20},{28,24},{5,1},{9,5},{13... | collective-permute-start | bytes 196616 | tf_op jit(solution)/shard_map/ppermute | solution.py:14
  126.5 107.0 %all-reduce.7.cloned.1.call-start = ((), (), s32[]{:S(2)}) async-start(), calls=%async_computation.3 | async-start | bytes 333824 | tf_op jit(solution)/shard_map/psum | solution.py:267
  132.9 113.3 %copy-start.8 = (f32[64,1024]{1,0:T(8,128)S(1)}, f32[64,1024]{1,0:T(8,128)}, u32[]{:S(2)}) copy-start(f32[64,1024]{1,0:T(8,128)} %custom-call.3) | copy-start | bytes 786436
  199.8 46.0 %all-to-all-start.1 = ((bf16[64,3,4,128]{3,0,1,2:T(8,128)(2,1)}), bf16[64,3,4,128]{3,0,1,2:T(8,128)(2,1)S(1)}, u32[]{:S(2)}, u32[]{:S(2)}) async-start(bf16[64,3,4,128]{3,0,1,2:T(8,128)(2,1)} %copy.54), calls=%async_computation.1 | async-start | bytes 393216 | tf_op jit(solution)/shard_map/all_to_all | solution.py:259
Sparse Core Ops, SparseCore 0:
  126.6 72.2 all-reduce.4
  201.9 31.4 all-reduce.6
